TPU v7x, 128 devices: a whole 4x4x4 slice. The times are simulated.
128 devices in a mesh: dp: 8 (over y, core), expert: 16 (over z, x).
Axes of the slice: x: 4, y: 4, z: 4, core: 2. Of those that a mesh axis runs over, the one named last changes fastest.
Arguments:
- tokens: bfloat16 [32768, 2048], P(('dp', 'expert')), may hold values from -6 to 6
- routes: int32 [32768, 2], P(('dp', 'expert')), may hold values from 0 to 31, all different within a row; in each aligned block of 256 rows (0 to 255, 256 to 511, ...) at most 32 rows name the same one
- gate_weights: float32 [32768, 2], P(('dp', 'expert')), may hold values from 0.2 to 1
- w_up: bfloat16 [32, 2048, 768], P('expert'), may hold values from -0.125 to 0.125
- w_down: bfloat16 [32, 768, 2048], P('expert'), may hold values from -0.21875 to 0.21875
- cotangent: bfloat16 [32768, 2048], P(('dp', 'expert')), may hold values from -6 to 6
Outputs:
- mixed: bfloat16 [32768, 2048], P(('dp', 'expert'))
- input_grad: bfloat16 [32768, 2048], P(('dp', 'expert'))
- up_grad: float32 [32, 2048, 768], P('expert', 'dp')
- down_grad: float32 [32, 768, 2048], P('expert', None, 'dp')
Inputs may be any that keep to these rules, and one draw needn't show every extreme that they name: Each row names 2 different experts. In the rows of one device no expert is named by more than 32 routes, and in every draw some expert is named by exactly 32 routes of some device.
All inputs are finite; a program needn't handle non-finite values.
Results may differ from a plain program's by a relative error of at most 0.015.
Values may be sent and summed in bfloat16 or wider, within the bound.
A program may use at most 192 MiB of HBM per device.

v0:
```python
import jax
import jax.numpy as jnp
from jax import lax
from jax.experimental import pallas as pl
from jax.experimental.pallas import tpu as pltpu
from jax.sharding import PartitionSpec as P

MESH = pl.DeviceIdType.MESH
SIDE = 4
CORES = 2
F32 = jnp.float32
BF16 = jnp.bfloat16


def dot(a, b, dims):
    return lax.dot_general(a, b, (dims, ((), ())), preferred_element_type=F32)


NN = ((1,), (0,))
NT = ((1,), (1,))
TN = ((0,), (0,))


def sigmoid(v):
    return 1.0 / (1.0 + jnp.exp(-v))


def step_of(j):
    return j ^ (j // 2)


def layer_kernel(
    tok_hbm, cot_hbm, routes, gates, wup_hbm, wdn_hbm,
    mixed_hbm, igrad_hbm, upg_hbm, dng_hbm,
    tokbuf, cotbuf, meta_z, meta_x, sbuf_t, sbuf_c, recv_t, recv_c, wu, wd,
    pre, act, dpre, ret_o, ret_d, rs, pmr, pdr, gst,
    load_sem, meta_sems, ag_send, ag_recv, meta_send, meta_recv,
    fwd_send, fwd_recv, bwd_send, bwd_recv, rs_send, rs_recv, part_send, part_recv, out_sem,
):
    dp, ex = lax.axis_index("dp"), lax.axis_index("expert")
    y, c = dp // CORES, dp % CORES
    z, x = ex // SIDE, ex % SIDE
    rows, width = tok_hbm.shape
    hidden = wup_hbm.shape[2]
    cap = rows // (SIDE * CORES)
    pair = CORES * cap
    tile = width // SIDE
    shard = width // (SIDE * CORES)
    line = SIDE * CORES
    mine = (x * CORES + c) * cap
    mine_z = (z * CORES + c) * cap

    def device(yy, cc, zz, xx):
        return (yy * CORES + cc, zz * SIDE + xx)

    def x_line(q):
        return (x + q // CORES) % SIDE, (c + q % CORES) % CORES

    def z_line(q):
        return (z + q // CORES) % SIDE, (c + q % CORES) % CORES

    def y_line(q):
        return (y + q // CORES) % SIDE, (c + q % CORES) % CORES

    def remote(src, dst, ssem, rsem, where):
        return pltpu.make_async_remote_copy(
            src_ref=src, dst_ref=dst, send_sem=ssem, recv_sem=rsem,
            device_id=where, device_id_type=MESH,
        )

    def await_bytes(ref, sem):
        pltpu.make_async_copy(ref, ref, sem).wait()

    tok_in = pltpu.make_async_copy(tok_hbm, tokbuf.at[z], load_sem.at[0])
    cot_in = pltpu.make_async_copy(cot_hbm, cotbuf.at[x], load_sem.at[1])
    wup_in = pltpu.make_async_copy(wup_hbm.at[c], wu, load_sem.at[2])
    wdn_in = pltpu.make_async_copy(wdn_hbm.at[c], wd, load_sem.at[3])
    tok_in.start()
    cot_in.start()

    barrier = pltpu.get_barrier_semaphore()

    def greet(where):
        pl.semaphore_signal(barrier, inc=1, device_id=where, device_id_type=MESH)

    @pl.loop(1, line)
    def _(q):
        xx, cc = x_line(q)
        greet(device(y, cc, z, xx))

    @pl.loop(CORES, line)
    def _(q):
        zz, cc = z_line(q)
        greet(device(y, cc, zz, x))
        yy, cc = y_line(q)
        greet(device(yy, cc, z, x))

    r0, r1 = routes[0:1, :], routes[1:2, :]
    experts = line * SIDE
    names = lax.broadcasted_iota(jnp.int32, (experts, rows), 0)
    hit0, hit1 = names == r0, names == r1
    onehot = jnp.where(hit0 | hit1, 1.0, 0.0).astype(BF16)
    earlier = (
        lax.broadcasted_iota(jnp.int32, (rows, rows), 0)
        < lax.broadcasted_iota(jnp.int32, (rows, rows), 1)
    )
    before = dot(onehot, jnp.where(earlier, 1.0, 0.0).astype(BF16), NN)
    slot0 = r0.astype(F32) * cap + jnp.sum(jnp.where(hit0, before, 0.0), axis=0, keepdims=True)
    slot1 = r1.astype(F32) * cap + jnp.sum(jnp.where(hit1, before, 0.0), axis=0, keepdims=True)
    meta = jnp.concatenate(
        [slot0, slot1, gates[0:1, :], gates[1:2, :], jnp.zeros((4, rows), F32)], axis=0
    )
    meta_z[z] = meta
    meta_x[x] = meta

    pl.semaphore_wait(barrier, line - 1 + 2 * (line - CORES))

    @pl.loop(1, SIDE)
    def _(j):
        d = step_of(j)
        to_z, to_x = device(y, c, (z + d) % SIDE, x), device(y, c, z, (x + d) % SIDE)
        remote(meta_z.at[z], meta_z.at[z], meta_send.at[0, d], meta_recv.at[0, z], to_z).start()
        remote(meta_x.at[x], meta_x.at[x], meta_send.at[1, d], meta_recv.at[1, x], to_x).start()

    tok_in.wait()
    cot_in.wait()

    @pl.loop(1, SIDE)
    def _(j):
        d = step_of(j)
        to_z, to_x = device(y, c, (z + d) % SIDE, x), device(y, c, z, (x + d) % SIDE)
        remote(tokbuf.at[z], tokbuf.at[z], ag_send.at[0, d], ag_recv.at[0, z], to_z).start()
        remote(cotbuf.at[x], cotbuf.at[x], ag_send.at[1, d], ag_recv.at[1, x], to_x).start()

    wup_in.start()
    wdn_in.start()

    place = lax.broadcasted_iota(jnp.int32, (rows, rows), 0)
    tok_slots = (place + z * rows).astype(F32)
    cot_slots = ((place // pair) * rows + x * pair + place % pair).astype(F32)

    @pl.loop(0, SIDE)
    def _(j):
        d = step_of(j)
        zs, xs = (z + d) % SIDE, (x + d) % SIDE

        @pl.when(j > 0)
        def _():
            await_bytes(meta_z.at[zs], meta_recv.at[0, zs])
            await_bytes(tokbuf.at[zs], ag_recv.at[0, zs])

        m = meta_z[zs]
        pick = jnp.where((tok_slots == m[0:1, :]) | (tok_slots == m[1:2, :]), 1.0, 0.0).astype(BF16)

        @pl.loop(0, SIDE)
        def _(n):
            cols = pl.ds(pl.multiple_of(n * tile, tile), tile)
            sbuf_t[zs, :, cols] = dot(pick, tokbuf[zs, :, cols], NN).astype(BF16)

        @pl.loop(1, line)
        def _(q):
            xx, cc = x_line(q)
            remote(
                sbuf_t.at[zs, pl.ds((xx * CORES + cc) * cap, cap)],
                recv_t.at[zs, pl.ds(mine, cap)],
                fwd_send.at[0, zs], fwd_recv.at[0, zs], device(y, cc, z, xx),
            ).start()

        pltpu.make_async_copy(
            sbuf_t.at[zs, pl.ds(mine, cap)], recv_t.at[zs, pl.ds(mine, cap)], fwd_recv.at[0, zs]
        ).start()

        @pl.when(j > 0)
        def _():
            await_bytes(meta_x.at[xs], meta_recv.at[1, xs])
            await_bytes(cotbuf.at[xs], ag_recv.at[1, xs])

        m = meta_x[xs]
        hit0, hit1 = cot_slots == m[0:1, :], cot_slots == m[1:2, :]
        pick = jnp.where(hit0 | hit1, 1.0, 0.0).astype(BF16)
        scale = jnp.sum(
            jnp.where(hit0, m[2:3, :], 0.0) + jnp.where(hit1, m[3:4, :], 0.0), axis=1, keepdims=True
        )

        @pl.loop(0, SIDE)
        def _(n):
            cols = pl.ds(pl.multiple_of(n * tile, tile), tile)
            sbuf_c[xs, :, cols] = (dot(pick, cotbuf[xs, :, cols], NN) * scale).astype(BF16)

        @pl.loop(1, line)
        def _(q):
            zz, cc = z_line(q)
            remote(
                sbuf_c.at[xs, pl.ds((zz * CORES + cc) * cap, cap)],
                recv_c.at[z, pl.ds((xs * CORES + c) * cap, cap)],
                fwd_send.at[1, xs], fwd_recv.at[1, xs], device(y, cc, zz, x),
            ).start()

        pltpu.make_async_copy(
            sbuf_c.at[xs, pl.ds(mine_z, cap)],
            recv_c.at[z, pl.ds((xs * CORES + c) * cap, cap)],
            fwd_recv.at[1, xs],
        ).start()

    wup_in.wait()
    wdn_in.wait()

    @pl.loop(0, SIDE)
    def _(j):
        zs = (z + step_of(j)) % SIDE
        await_bytes(recv_t.at[zs], fwd_recv.at[0, zs])
        v = dot(recv_t[zs], wu[...], NN)
        pre[zs] = v
        a = (v * sigmoid(v)).astype(BF16)
        act[zs] = a
        await_bytes(sbuf_t.at[zs, pl.ds(0, rows - cap)], fwd_send.at[0, zs])

        @pl.loop(0, SIDE)
        def _(n):
            cols = pl.ds(pl.multiple_of(n * tile, tile), tile)
            sbuf_t[zs, :, cols] = dot(act[zs], wd[:, cols], NN).astype(BF16)

        @pl.loop(1, line)
        def _(q):
            xx, cc = x_line(q)
            remote(
                sbuf_t.at[zs, pl.ds((xx * CORES + cc) * cap, cap)],
                ret_o.at[zs, pl.ds(mine, cap)],
                bwd_send.at[0, zs], bwd_recv.at[0, zs], device(y, cc, z, xx),
            ).start()

        pltpu.make_async_copy(
            sbuf_t.at[zs, pl.ds(mine, cap)], ret_o.at[zs, pl.ds(mine, cap)], bwd_recv.at[0, zs]
        ).start()

    @pl.loop(0, SIDE)
    def _(j):
        xs = (x + step_of(j)) % SIDE
        part = pl.ds(pl.multiple_of(xs * pair, pair), pair)
        await_bytes(recv_c.at[:, part], fwd_recv.at[1, xs])
        da = dot(recv_c[:, part, :].reshape(rows, width), wd[...], NT)
        v = pre[:, part, :].reshape(rows, hidden)
        s = sigmoid(v)
        dp_rows = (da * s * (1.0 + v * (1.0 - s))).astype(BF16)
        dpre[:, part, :] = dp_rows.reshape(SIDE, pair, hidden)
        await_bytes(sbuf_c.at[xs, pl.ds(0, rows - cap)], fwd_send.at[1, xs])

        @pl.loop(0, SIDE)
        def _(n):
            cols = pl.ds(pl.multiple_of(n * tile, tile), tile)
            left = dpre[:, part, :].reshape(rows, hidden)
            sbuf_c[xs, :, cols] = dot(left, wu[cols, :], NT).astype(BF16)

        @pl.loop(1, line)
        def _(q):
            zz, cc = z_line(q)
            remote(
                sbuf_c.at[xs, pl.ds((zz * CORES + cc) * cap, cap)],
                ret_d.at[xs, pl.ds(mine_z, cap)],
                bwd_send.at[1, xs], bwd_recv.at[1, xs], device(y, cc, zz, x),
            ).start()

        pltpu.make_async_copy(
            sbuf_c.at[xs, pl.ds(mine_z, cap)], ret_d.at[xs, pl.ds(mine_z, cap)], bwd_recv.at[1, xs]
        ).start()

    @pl.loop(1, SIDE)
    def _(d):
        for k, buf, own, metas in ((0, tokbuf, z, meta_z), (1, cotbuf, x, meta_x)):
            await_bytes(buf.at[own], ag_send.at[k, d])
            await_bytes(metas.at[own], meta_send.at[k, d])

    thirds = hidden // rows
    for g, left, right, gbuf in ((0, act, recv_c, cotbuf), (1, dpre, recv_t, tokbuf)):

        @pl.loop(0, SIDE)
        def _(n, g=g, left=left, right=right, gbuf=gbuf):
            yy = (y + step_of(SIDE - 1 - n)) % SIDE
            cols = pl.ds(pl.multiple_of(yy * tile, tile), tile)
            r = dot(
                left[...].reshape(SIDE * rows, hidden),
                right[:, :, cols].reshape(SIDE * rows, tile),
                TN,
            )
            gbuf[0:thirds, :, cols] = r.astype(BF16).reshape(thirds, rows, tile)

        @pl.loop(1, line)
        def _(q, g=g, gbuf=gbuf):
            yy, cc = y_line(line - q)
            cols = pl.ds(pl.multiple_of((yy * CORES + cc) * shard, shard), shard)
            remote(
                gbuf.at[0:thirds, :, cols], rs.at[g, c, y], rs_send.at[g], rs_recv.at[g],
                device(yy, cc, z, x),
            ).start()

        cols = pl.ds(pl.multiple_of((y * CORES + c) * shard, shard), shard)
        pltpu.make_async_copy(gbuf.at[0:thirds, :, cols], rs.at[g, c, y], rs_recv.at[g]).start()

    def shares(k, own, slots, metas, ret, send, got, out_hbm, weighted):
        def picks(m):
            hit0, hit1 = slots == m[0:1, :], slots == m[1:2, :]
            if not weighted:
                return [jnp.where(hit0 | hit1, 1.0, 0.0).astype(BF16)]
            g = jnp.where(hit0, m[2:3, :], 0.0) + jnp.where(hit1, m[3:4, :], 0.0)
            high = g.astype(BF16)
            return [high, (g - high.astype(F32)).astype(BF16)]

        @pl.loop(1, SIDE)
        def _(j):
            src = (own + step_of(j)) % SIDE
            await_bytes(ret.at[src], bwd_recv.at[k, src])
            weights = picks(metas[src])

            @pl.loop(0, SIDE)
            def _(n):
                cols = pl.ds(pl.multiple_of(n * tile, tile), tile)
                v = ret[src, :, cols]
                send[src, :, cols] = sum(dot(w, v, TN) for w in weights).astype(BF16)

            where = device(y, c, src, x) if k == 0 else device(y, c, z, src)
            slot = (own - src + SIDE - 1) % SIDE
            remote(send.at[src], got.at[slot], part_send.at[k, src], part_recv.at[k, slot], where).start()

    def finish(k, own, slots, metas, ret, send, got, out_hbm, weighted):
        await_bytes(ret.at[own], bwd_recv.at[k, own])
        m = metas[own]
        hit0, hit1 = slots == m[0:1, :], slots == m[1:2, :]
        if weighted:
            g = jnp.where(hit0, m[2:3, :], 0.0) + jnp.where(hit1, m[3:4, :], 0.0)
            high = g.astype(BF16)
            weights = [high, (g - high.astype(F32)).astype(BF16)]
        else:
            weights = [jnp.where(hit0 | hit1, 1.0, 0.0).astype(BF16)]

        @pl.loop(0, SIDE - 1)
        def _(slot):
            await_bytes(got.at[slot], part_recv.at[k, slot])

        @pl.loop(0, SIDE)
        def _(n):
            cols = pl.ds(pl.multiple_of(n * tile, tile), tile)
            v = ret[own, :, cols]
            total = sum(dot(w, v, TN) for w in weights)
            for slot in range(SIDE - 1):
                total = total + got[slot, :, cols].astype(F32)
            send[own, :, cols] = total.astype(BF16)

        pltpu.make_async_copy(send.at[own], out_hbm, out_sem.at[k]).start()

    fwd = (0, z, tok_slots, meta_z, ret_o, recv_t, pmr, mixed_hbm, True)
    bwd = (1, x, cot_slots, meta_x, ret_d, recv_c, pdr, igrad_hbm, False)
    shares(*fwd)
    shares(*bwd)
    finish(*fwd)

    await_bytes(rs.at[0], rs_recv.at[0])

    @pl.loop(0, CORES)
    def _(e):
        total = rs[0, e, 0].astype(F32)
        for yy in range(1, SIDE):
            total = total + rs[0, e, yy].astype(F32)
        gst[e] = total.reshape(hidden, shard)

    pltpu.make_async_copy(gst, dng_hbm, out_sem.at[2]).start()
    await_bytes(rs.at[1], rs_recv.at[1])

    @pl.loop(0, CORES)
    def _(e):
        total = rs[1, e, 0].astype(F32)
        for yy in range(1, SIDE):
            total = total + rs[1, e, yy].astype(F32)
        pre[e] = total.reshape(hidden, shard).T

    pltpu.make_async_copy(pre.at[0:CORES], upg_hbm, out_sem.at[3]).start()
    finish(*bwd)

    @pl.loop(0, SIDE)
    def _(j):
        for k, buf in ((0, sbuf_t), (1, sbuf_c)):
            await_bytes(buf.at[j, pl.ds(0, rows - cap)], bwd_send.at[k, j])

    @pl.loop(1, SIDE)
    def _(d):
        for k, own, buf in ((0, z, recv_t), (1, x, recv_c)):
            src = (own + d) % SIDE
            await_bytes(buf.at[src], part_send.at[k, src])

    for g, gbuf in ((0, cotbuf), (1, tokbuf)):
        await_bytes(gbuf.at[0:thirds, :, 0 : width - shard], rs_send.at[g])

    pltpu.make_async_copy(recv_t.at[z], mixed_hbm, out_sem.at[0]).wait()
    pltpu.make_async_copy(recv_c.at[x], igrad_hbm, out_sem.at[1]).wait()
    pltpu.make_async_copy(gst, dng_hbm, out_sem.at[2]).wait()
    pltpu.make_async_copy(pre.at[0:CORES], upg_hbm, out_sem.at[3]).wait()


def on_device(tokens, routes, gate_weights, w_up, w_down, cotangent):
    rows, width = tokens.shape
    held, _, hidden = w_up.shape
    shard = width // (SIDE * CORES)
    hbm = pl.BlockSpec(memory_space=pl.ANY)
    vmem = pl.BlockSpec(memory_space=pltpu.VMEM)
    four = pltpu.VMEM((SIDE, rows, width), BF16)
    three = pltpu.VMEM((SIDE - 1, rows, width), BF16)
    dma = pltpu.SemaphoreType.DMA
    mixed, igrad, upg, dng = pl.pallas_call(
        layer_kernel,
        out_shape=(
            jax.ShapeDtypeStruct((rows, width), BF16),
            jax.ShapeDtypeStruct((rows, width), BF16),
            jax.ShapeDtypeStruct((held, shard, hidden), F32),
            jax.ShapeDtypeStruct((held, hidden, shard), F32),
        ),
        in_specs=[hbm, hbm, vmem, vmem, hbm, hbm],
        out_specs=(hbm, hbm, hbm, hbm),
        scratch_shapes=[
            four, four,
            pltpu.VMEM((SIDE, 8, rows), F32), pltpu.VMEM((SIDE, 8, rows), F32),
            four, four, four, four,
            pltpu.VMEM((width, hidden), BF16), pltpu.VMEM((hidden, width), BF16),
            pltpu.VMEM((SIDE, rows, hidden), F32),
            pltpu.VMEM((SIDE, rows, hidden), BF16), pltpu.VMEM((SIDE, rows, hidden), BF16),
            four, four,
            pltpu.VMEM((2, CORES, SIDE, hidden // rows, rows, shard), BF16),
            three, three,
            pltpu.VMEM((CORES, hidden, shard), F32),
            dma((4,)), dma((2,)),
            dma((2, SIDE)), dma((2, SIDE)), dma((2, SIDE)), dma((2, SIDE)),
            dma((2, SIDE)), dma((2, SIDE)), dma((2, SIDE)), dma((2, SIDE)),
            dma((2,)), dma((2,)), dma((2, SIDE)), dma((2, SIDE)), dma((4,)),
        ],
        compiler_params=pltpu.CompilerParams(
            collective_id=0, has_side_effects=True, vmem_limit_bytes=63 << 20
        ),
    )(tokens, cotangent, routes.T, gate_weights.T, w_up, w_down)
    return (mixed, igrad, upg, dng)


def solution(mesh):
    rows = P(("dp", "expert"), None)
    held = P("expert", None, None)
    return jax.shard_map(
        on_device,
        mesh=mesh,
        in_specs=(rows, rows, rows, held, held, rows),
        out_specs=(rows, rows, P("expert", "dp", None), P("expert", None, "dp")),
        check_vma=False,
    )
```

profile of v0, /device:TPU:1, one launch (start us, length us, event | category | flops | bytes accessed | tf_op | source)
XLA Modules:
  0.0 213.5 jit_solution(6491452217597109178)
XLA Ops:
  0.6 205.5 %shard_map.93 = (bf16[256,2048]{1,0:T(8,128)(2,1)}, bf16[256,2048]{1,0:T(8,128)(2,1)}, f32[2,256,768]{2,1,0:T(8,128)}, f32[2,768,256]{2,1,0:T(8,128)}) custom-call(bf16[256,2048]{1,0:T(8,128)(2,1)} %tok_hbm.1, bf16[256,2048]{1,0:T(8,128)(2,1)} %cot_hbm.1, s32[2,256]{1,0:T(2,128)} %bitcast.2, f32[2,256]{1,0:T(2,128)} %bitcast.3, ...), custom_call_target="tpu_custom_call" | custom-call | tf_op jit(solution)/shard_map/pallas_call | solution.py:407
  206.2 0.0 copy-start.2
  206.2 2.4 %copy.14 = bf16[256,2048]{1,0:T(8,128)(2,1)} copy(bf16[256,2048]{1,0:T(8,128)(2,1)} %get-tuple-element.8) | data formatting | bytes 2097152
  208.6 0.0 copy-done.2
  208.6 0.0 copy-start.1
  208.6 1.0 copy.15
  209.6 0.8 copy-done.1
  210.4 0.0 copy-start
  210.4 1.1 copy.16
  211.5 0.8 copy-done
  212.4 1.1 copy.17
Async XLA Ops:
  206.2 2.4 %copy-start.2 = (bf16[256,2048]{1,0:T(8,128)(2,1)S(1)}, bf16[256,2048]{1,0:T(8,128)(2,1)}, u32[]{:S(2)}) copy-start(bf16[256,2048]{1,0:T(8,128)(2,1)} %get-tuple-element.9) | copy-start | bytes 3145732
  208.6 1.8 copy-start.1
  210.4 2.0 copy-start
where the time goes:
time: 214 us
  Pallas kernels  206 us (96%)
  local copies, waits for them, and re-layouts  7.3 us (3%)
    pallas_call x1, Pallas kernels, on_device(): pl.pallas_call(layer_kernel, out_shape=(jax.ShapeDtypeStruct((rows, width...  206 us
    unnamed x10, local copies, waits for them, and re-layouts  7.3 us

commit v1 on v0

--- a/solution.py
+++ b/solution.py
@@ -34,7 +34,7 @@
     mixed_hbm, igrad_hbm, upg_hbm, dng_hbm,
     tokbuf, cotbuf, meta_z, meta_x, sbuf_t, sbuf_c, recv_t, recv_c, wu, wd,
     pre, act, dpre, ret_o, ret_d, rs, pmr, pdr, gst,
-    load_sem, meta_sems, ag_send, ag_recv, meta_send, meta_recv,
+    load_sem, ag_send, ag_recv, hand_send, meta_send, meta_recv,
     fwd_send, fwd_recv, bwd_send, bwd_recv, rs_send, rs_recv, part_send, part_recv, out_sem,
 ):
     dp, ex = lax.axis_index("dp"), lax.axis_index("expert")
@@ -67,6 +67,14 @@
             src_ref=src, dst_ref=dst, send_sem=ssem, recv_sem=rsem,
             device_id=where, device_id_type=MESH,
         )
+
+    half = rows // 2
+    halves = (pl.ds(0, half), pl.ds(half, half))
+
+    def near(k, d):
+        if k == 0:
+            return device(y, c, (z + d) % SIDE, x)
+        return device(y, c, z, (x + d) % SIDE)
 
     def await_bytes(ref, sem):
         pltpu.make_async_copy(ref, ref, sem).wait()
@@ -125,12 +133,13 @@
     tok_in.wait()
     cot_in.wait()
 
-    @pl.loop(1, SIDE)
-    def _(j):
-        d = step_of(j)
-        to_z, to_x = device(y, c, (z + d) % SIDE, x), device(y, c, z, (x + d) % SIDE)
-        remote(tokbuf.at[z], tokbuf.at[z], ag_send.at[0, d], ag_recv.at[0, z], to_z).start()
-        remote(cotbuf.at[x], cotbuf.at[x], ag_send.at[1, d], ag_recv.at[1, x], to_x).start()
+    axes = ((0, tokbuf, z), (1, cotbuf, x))
+    for first in (True, False):
+        for k, buf, own in axes:
+            for side, d in ((0, 1), (1, SIDE - 1)):
+                h = side if first else 1 - side
+                part = buf.at[own, halves[h]]
+                remote(part, part, ag_send.at[k, side, h], ag_recv.at[k, own, h], near(k, d)).start()
 
     wup_in.start()
     wdn_in.start()
@@ -144,11 +153,29 @@
         d = step_of(j)
         zs, xs = (z + d) % SIDE, (x + d) % SIDE
 
-        @pl.when(j > 0)
+        @pl.when(j == 1)
         def _():
-            await_bytes(meta_z.at[zs], meta_recv.at[0, zs])
-            await_bytes(tokbuf.at[zs], ag_recv.at[0, zs])
-
+            for k, buf, own in axes:
+                for side, back, ahead in ((0, SIDE - 1, 1), (1, 1, SIDE - 1)):
+                    src = (own + back) % SIDE
+                    part = buf.at[src, halves[side]]
+                    await_bytes(part, ag_recv.at[k, src, side])
+                    remote(part, part, hand_send.at[k, side], ag_recv.at[k, src, side], near(k, ahead)).start()
+
+        def arrived(k, buf, metas, src):
+            @pl.when(j > 0)
+            def _():
+                await_bytes(metas.at[src], meta_recv.at[k, src])
+
+            @pl.when((d == 1) | (d == 2))
+            def _():
+                await_bytes(buf.at[src, halves[0]], ag_recv.at[k, src, 0])
+
+            @pl.when((d == SIDE - 1) | (d == 2))
+            def _():
+                await_bytes(buf.at[src, halves[1]], ag_recv.at[k, src, 1])
+
+        arrived(0, tokbuf, meta_z, zs)
         m = meta_z[zs]
         pick = jnp.where((tok_slots == m[0:1, :]) | (tok_slots == m[1:2, :]), 1.0, 0.0).astype(BF16)
 
@@ -170,11 +197,7 @@
             sbuf_t.at[zs, pl.ds(mine, cap)], recv_t.at[zs, pl.ds(mine, cap)], fwd_recv.at[0, zs]
         ).start()
 
-        @pl.when(j > 0)
-        def _():
-            await_bytes(meta_x.at[xs], meta_recv.at[1, xs])
-            await_bytes(cotbuf.at[xs], ag_recv.at[1, xs])
-
+        arrived(1, cotbuf, meta_x, xs)
         m = meta_x[xs]
         hit0, hit1 = cot_slots == m[0:1, :], cot_slots == m[1:2, :]
         pick = jnp.where(hit0 | hit1, 1.0, 0.0).astype(BF16)
@@ -266,9 +289,14 @@
 
     @pl.loop(1, SIDE)
     def _(d):
-        for k, buf, own, metas in ((0, tokbuf, z, meta_z), (1, cotbuf, x, meta_x)):
-            await_bytes(buf.at[own], ag_send.at[k, d])
+        for k, own, metas in ((0, z, meta_z), (1, x, meta_x)):
             await_bytes(metas.at[own], meta_send.at[k, d])
+
+    for k, buf, own in axes:
+        for side, back in ((0, SIDE - 1), (1, 1)):
+            for h in range(2):
+                await_bytes(buf.at[own, halves[h]], ag_send.at[k, side, h])
+            await_bytes(buf.at[(own + back) % SIDE, halves[side]], hand_send.at[k, side])
 
     thirds = hidden // rows
     for g, left, right, gbuf in ((0, act, recv_c, cotbuf), (1, dpre, recv_t, tokbuf)):
@@ -296,61 +324,81 @@
         cols = pl.ds(pl.multiple_of((y * CORES + c) * shard, shard), shard)
         pltpu.make_async_copy(gbuf.at[0:thirds, :, cols], rs.at[g, c, y], rs_recv.at[g]).start()
 
-    def shares(k, own, slots, metas, ret, send, got, out_hbm, weighted):
-        def picks(m):
-            hit0, hit1 = slots == m[0:1, :], slots == m[1:2, :]
+    def share(k, own, slots, metas, ret, weighted):
+        def of(src, h, cols):
+            m = metas[src]
+            m = m[:, h * half : (h + 1) * half]
+            hit0, hit1 = slots[:, 0:half] == m[0:1, :], slots[:, 0:half] == m[1:2, :]
+            v = ret[src, :, cols]
             if not weighted:
-                return [jnp.where(hit0 | hit1, 1.0, 0.0).astype(BF16)]
+                return dot(jnp.where(hit0 | hit1, 1.0, 0.0).astype(BF16), v, TN)
             g = jnp.where(hit0, m[2:3, :], 0.0) + jnp.where(hit1, m[3:4, :], 0.0)
             high = g.astype(BF16)
-            return [high, (g - high.astype(F32)).astype(BF16)]
-
-        @pl.loop(1, SIDE)
-        def _(j):
-            src = (own + step_of(j)) % SIDE
-            await_bytes(ret.at[src], bwd_recv.at[k, src])
-            weights = picks(metas[src])
-
-            @pl.loop(0, SIDE)
-            def _(n):
-                cols = pl.ds(pl.multiple_of(n * tile, tile), tile)
-                v = ret[src, :, cols]
-                send[src, :, cols] = sum(dot(w, v, TN) for w in weights).astype(BF16)
-
-            where = device(y, c, src, x) if k == 0 else device(y, c, z, src)
-            slot = (own - src + SIDE - 1) % SIDE
-            remote(send.at[src], got.at[slot], part_send.at[k, src], part_recv.at[k, slot], where).start()
-
-    def finish(k, own, slots, metas, ret, send, got, out_hbm, weighted):
-        await_bytes(ret.at[own], bwd_recv.at[k, own])
-        m = metas[own]
-        hit0, hit1 = slots == m[0:1, :], slots == m[1:2, :]
-        if weighted:
-            g = jnp.where(hit0, m[2:3, :], 0.0) + jnp.where(hit1, m[3:4, :], 0.0)
-            high = g.astype(BF16)
-            weights = [high, (g - high.astype(F32)).astype(BF16)]
-        else:
-            weights = [jnp.where(hit0 | hit1, 1.0, 0.0).astype(BF16)]
-
-        @pl.loop(0, SIDE - 1)
-        def _(slot):
-            await_bytes(got.at[slot], part_recv.at[k, slot])
-
+            low = (g - high.astype(F32)).astype(BF16)
+            return dot(high, v, TN) + dot(low, v, TN)
+        return of
+
+    def tiles(body):
         @pl.loop(0, SIDE)
         def _(n):
-            cols = pl.ds(pl.multiple_of(n * tile, tile), tile)
-            v = ret[own, :, cols]
-            total = sum(dot(w, v, TN) for w in weights)
-            for slot in range(SIDE - 1):
-                total = total + got[slot, :, cols].astype(F32)
-            send[own, :, cols] = total.astype(BF16)
-
+            body(pl.ds(pl.multiple_of(n * tile, tile), tile))
+
+    def pass_on(k, send, got, src, h, slot, where_d):
+        part = send.at[src, halves[h]]
+        remote(part, got.at[slot, halves[h]], part_send.at[k, slot, h], part_recv.at[k, slot, h], near(k, where_d)).start()
+
+    def shares(k, own, slots, metas, ret, send, got, out_hbm, weighted):
+        of = share(k, own, slots, metas, ret, weighted)
+        ahead, behind, far = (own + 1) % SIDE, (own + SIDE - 1) % SIDE, (own + 2) % SIDE
+        for src, h, slot, d in ((ahead, 1, 1, 1), (behind, 0, 0, SIDE - 1)):
+            await_bytes(ret.at[src], bwd_recv.at[k, src])
+
+            def body(cols, src=src, h=h):
+                send[src, halves[h], cols] = of(src, h, cols).astype(BF16)
+
+            tiles(body)
+            pass_on(k, send, got, src, h, slot, d)
+        await_bytes(ret.at[far], bwd_recv.at[k, far])
+        for h, d in ((0, 1), (1, SIDE - 1)):
+            def body(cols, h=h):
+                send[far, halves[h], cols] = of(far, h, cols).astype(BF16)
+
+            tiles(body)
+            pass_on(k, send, got, far, h, 2, d)
+
+    def hand_on(k, own, slots, metas, ret, send, got, out_hbm, weighted):
+        of = share(k, own, slots, metas, ret, weighted)
+        ahead, behind = (own + 1) % SIDE, (own + SIDE - 1) % SIDE
+        for src, h, slot, d in ((ahead, 0, 1, 1), (behind, 1, 0, SIDE - 1)):
+            await_bytes(got.at[2, halves[h]], part_recv.at[k, 2, h])
+
+            def body(cols, src=src, h=h):
+                total = of(src, h, cols) + got[2, halves[h], cols].astype(F32)
+                send[src, halves[h], cols] = total.astype(BF16)
+
+            tiles(body)
+            pass_on(k, send, got, src, h, slot, d)
+
+    def finish(k, own, slots, metas, ret, send, got, out_hbm, weighted):
+        of = share(k, own, slots, metas, ret, weighted)
+        await_bytes(ret.at[own], bwd_recv.at[k, own])
+        for slot in range(2):
+            for h in range(2):
+                await_bytes(got.at[slot, halves[h]], part_recv.at[k, slot, h])
+        for h in range(2):
+            def body(cols, h=h):
+                total = of(own, h, cols) + got[0, halves[h], cols].astype(F32)
+                send[own, halves[h], cols] = (total + got[1, halves[h], cols].astype(F32)).astype(BF16)
+
+            tiles(body)
         pltpu.make_async_copy(send.at[own], out_hbm, out_sem.at[k]).start()
 
     fwd = (0, z, tok_slots, meta_z, ret_o, recv_t, pmr, mixed_hbm, True)
     bwd = (1, x, cot_slots, meta_x, ret_d, recv_c, pdr, igrad_hbm, False)
     shares(*fwd)
     shares(*bwd)
+    hand_on(*fwd)
+    hand_on(*bwd)
     finish(*fwd)
 
     await_bytes(rs.at[0], rs_recv.at[0])
@@ -380,11 +428,10 @@
         for k, buf in ((0, sbuf_t), (1, sbuf_c)):
             await_bytes(buf.at[j, pl.ds(0, rows - cap)], bwd_send.at[k, j])
 
-    @pl.loop(1, SIDE)
-    def _(d):
-        for k, own, buf in ((0, z, recv_t), (1, x, recv_c)):
-            src = (own + d) % SIDE
-            await_bytes(buf.at[src], part_send.at[k, src])
+    for k, got in ((0, pmr), (1, pdr)):
+        for slot in range(SIDE - 1):
+            for h in range(2):
+                await_bytes(got.at[slot, halves[h]], part_send.at[k, slot, h])
 
     for g, gbuf in ((0, cotbuf), (1, tokbuf)):
         await_bytes(gbuf.at[0:thirds, :, 0 : width - shard], rs_send.at[g])
@@ -393,6 +440,21 @@
     pltpu.make_async_copy(recv_c.at[x], igrad_hbm, out_sem.at[1]).wait()
     pltpu.make_async_copy(gst, dng_hbm, out_sem.at[2]).wait()
     pltpu.make_async_copy(pre.at[0:CORES], upg_hbm, out_sem.at[3]).wait()
+
+
+def copy_kernel(*refs):
+    srcs, dsts, bufs, sem = refs[0:4], refs[4:8], refs[8:12], refs[12]
+    pieces = []
+    for i in range(4):
+        first = srcs[i].shape[0] // 2
+        pieces += [(i, h, pl.ds(h * first, first)) for h in range(2)]
+    for i, h, part in pieces:
+        pltpu.make_async_copy(srcs[i].at[part], bufs[i].at[part], sem.at[0, i, h]).start()
+    for i, h, part in pieces:
+        pltpu.make_async_copy(srcs[i].at[part], bufs[i].at[part], sem.at[0, i, h]).wait()
+        pltpu.make_async_copy(bufs[i].at[part], dsts[i].at[part], sem.at[1, i, h]).start()
+    for i, h, part in pieces:
+        pltpu.make_async_copy(bufs[i].at[part], dsts[i].at[part], sem.at[1, i, h]).wait()
 
 
 def on_device(tokens, routes, gate_weights, w_up, w_down, cotangent):
@@ -404,7 +466,7 @@
     four = pltpu.VMEM((SIDE, rows, width), BF16)
     three = pltpu.VMEM((SIDE - 1, rows, width), BF16)
     dma = pltpu.SemaphoreType.DMA
-    mixed, igrad, upg, dng = pl.pallas_call(
+    results = pl.pallas_call(
         layer_kernel,
         out_shape=(
             jax.ShapeDtypeStruct((rows, width), BF16),
@@ -425,16 +487,22 @@
             pltpu.VMEM((2, CORES, SIDE, hidden // rows, rows, shard), BF16),
             three, three,
             pltpu.VMEM((CORES, hidden, shard), F32),
-            dma((4,)), dma((2,)),
+            dma((4,)), dma((2, 2, 2)), dma((2, SIDE, 2)), dma((2, 2)),
+            dma((2, SIDE)), dma((2, SIDE)),
             dma((2, SIDE)), dma((2, SIDE)), dma((2, SIDE)), dma((2, SIDE)),
-            dma((2, SIDE)), dma((2, SIDE)), dma((2, SIDE)), dma((2, SIDE)),
-            dma((2,)), dma((2,)), dma((2, SIDE)), dma((2, SIDE)), dma((4,)),
+            dma((2,)), dma((2,)), dma((2, SIDE - 1, 2)), dma((2, SIDE - 1, 2)), dma((4,)),
         ],
         compiler_params=pltpu.CompilerParams(
             collective_id=0, has_side_effects=True, vmem_limit_bytes=63 << 20
         ),
     )(tokens, cotangent, routes.T, gate_weights.T, w_up, w_down)
-    return (mixed, igrad, upg, dng)
+    return pl.pallas_call(
+        copy_kernel,
+        out_shape=tuple(jax.ShapeDtypeStruct(r.shape, r.dtype) for r in results),
+        in_specs=[hbm] * 4,
+        out_specs=(hbm,) * 4,
+        scratch_shapes=[pltpu.VMEM(r.shape, r.dtype) for r in results] + [dma((2, 4, 2))],
+    )(*results)
 
 
 def solution(mesh):

time: 214 us -> 192 us (0.90)
  Pallas kernels: 206 us -> 192 us
  local copies, waits for them, and re-layouts: 7.3 us -> 0 us
    pallas_call x1, Pallas kernels: 206 us -> 187 us  [on_device(): pl.pallas_call(layer_kernel, out_shape=(jax.ShapeDtypeStruct((rows, width...]
    unnamed x10 -> x0, local copies, waits for them, and re-layouts: 7.3 us -> none
    pallas_call x0 -> x1, Pallas kernels: none -> 4.78 us  [on_device(): pl.pallas_call(copy_kernel, out_shape=tuple((jax.ShapeDtypeStruct(r.shape...]
where the time goes in v1:
time: 192 us
  Pallas kernels  192 us (100%)
    pallas_call x1, Pallas kernels, on_device(): pl.pallas_call(layer_kernel, out_shape=(jax.ShapeDtypeStruct((rows, width...  187 us
    pallas_call x1, Pallas kernels, on_device(): pl.pallas_call(copy_kernel, out_shape=tuple((jax.ShapeDtypeStruct(r.shape...  4.78 us

profile of v1, /device:TPU:1, one launch (start us, length us, event | category | flops | bytes accessed | tf_op | source)
XLA Modules:
  0.0 192.2 jit_solution(3457399174980740628)
XLA Ops:
  0.6 186.8 %shard_map.93 = (bf16[256,2048]{1,0:T(8,128)(2,1)}, bf16[256,2048]{1,0:T(8,128)(2,1)}, f32[2,256,768]{2,1,0:T(8,128)}, f32[2,768,256]{2,1,0:T(8,128)}) custom-call(bf16[256,2048]{1,0:T(8,128)(2,1)} %tok_hbm.1, bf16[256,2048]{1,0:T(8,128)(2,1)} %cot_hbm.1, s32[2,256]{1,0:T(2,128)} %bitcast.2, f32[2,256]{1,0:T(2,128)} %bitcast.3, ...), custom_call_target="tpu_custom_call" | custom-call | tf_op jit(solution)/shard_map/pallas_call | solution.py:469
  187.5 4.8 %shard_map.94 = (bf16[256,2048]{1,0:T(8,128)(2,1)}, bf16[256,2048]{1,0:T(8,128)(2,1)}, f32[2,256,768]{2,1,0:T(8,128)}, f32[2,768,256]{2,1,0:T(8,128)}) custom-call(bf16[256,2048]{1,0:T(8,128)(2,1)} %get-tuple-element.8.refs_0_, bf16[256,2048]{1,0:T(8,128)(2,1)} %get-tuple-element.9.refs_1_, f32[2,256,768]{2,1,0:T(8,128)} %get-tuple-element.10.refs_2_, ...), custom_call_target="tpu_custom_call" | custom-call | tf_op jit(solution)/shard_map/pallas_call | solution.py:499

commit v2 on v1

--- a/solution.py
+++ b/solution.py
@@ -34,7 +34,7 @@
     mixed_hbm, igrad_hbm, upg_hbm, dng_hbm,
     tokbuf, cotbuf, meta_z, meta_x, sbuf_t, sbuf_c, recv_t, recv_c, wu, wd,
     pre, act, dpre, ret_o, ret_d, rs, pmr, pdr, gst,
-    load_sem, ag_send, ag_recv, hand_send, meta_send, meta_recv,
+    load_sem, ag_send, ag_recv, hand_send, meta_send, meta_recv, fwd_own,
     fwd_send, fwd_recv, bwd_send, bwd_recv, rs_send, rs_recv, part_send, part_recv, out_sem,
 ):
     dp, ex = lax.axis_index("dp"), lax.axis_index("expert")
@@ -148,56 +148,58 @@
     tok_slots = (place + z * rows).astype(F32)
     cot_slots = ((place // pair) * rows + x * pair + place % pair).astype(F32)
 
-    @pl.loop(0, SIDE)
-    def _(j):
-        d = step_of(j)
-        zs, xs = (z + d) % SIDE, (x + d) % SIDE
-
-        @pl.when(j == 1)
-        def _():
-            for k, buf, own in axes:
-                for side, back, ahead in ((0, SIDE - 1, 1), (1, 1, SIDE - 1)):
-                    src = (own + back) % SIDE
-                    part = buf.at[src, halves[side]]
-                    await_bytes(part, ag_recv.at[k, src, side])
-                    remote(part, part, hand_send.at[k, side], ag_recv.at[k, src, side], near(k, ahead)).start()
-
-        def arrived(k, buf, metas, src):
-            @pl.when(j > 0)
-            def _():
-                await_bytes(metas.at[src], meta_recv.at[k, src])
-
-            @pl.when((d == 1) | (d == 2))
-            def _():
-                await_bytes(buf.at[src, halves[0]], ag_recv.at[k, src, 0])
-
-            @pl.when((d == SIDE - 1) | (d == 2))
-            def _():
-                await_bytes(buf.at[src, halves[1]], ag_recv.at[k, src, 1])
-
-        arrived(0, tokbuf, meta_z, zs)
+    def tiles(body):
+        @pl.loop(0, SIDE)
+        def _(n):
+            body(pl.ds(pl.multiple_of(n * tile, tile), tile))
+
+    def hand_over():
+        for k, buf, own in axes:
+            for side, back, ahead in ((0, SIDE - 1, 1), (1, 1, SIDE - 1)):
+                src = (own + back) % SIDE
+                part = buf.at[src, halves[side]]
+                await_bytes(part, ag_recv.at[k, src, side])
+                remote(part, part, hand_send.at[k, side], ag_recv.at[k, src, side], near(k, ahead)).start()
+
+    def arrived(k, buf, metas, src, d):
+        if d != 0:
+            await_bytes(metas.at[src], meta_recv.at[k, src])
+        if d in (1, 2):
+            await_bytes(buf.at[src, halves[0]], ag_recv.at[k, src, 0])
+        if d in (SIDE - 1, 2):
+            await_bytes(buf.at[src, halves[1]], ag_recv.at[k, src, 1])
+
+    def relay_tokens(d):
+        zs = (z + d) % SIDE
+        arrived(0, tokbuf, meta_z, zs, d)
         m = meta_z[zs]
         pick = jnp.where((tok_slots == m[0:1, :]) | (tok_slots == m[1:2, :]), 1.0, 0.0).astype(BF16)
 
-        @pl.loop(0, SIDE)
-        def _(n):
-            cols = pl.ds(pl.multiple_of(n * tile, tile), tile)
+        def body(cols):
             sbuf_t[zs, :, cols] = dot(pick, tokbuf[zs, :, cols], NN).astype(BF16)
 
-        @pl.loop(1, line)
-        def _(q):
+        tiles(body)
+
+        def send(q, sem):
             xx, cc = x_line(q)
             remote(
                 sbuf_t.at[zs, pl.ds((xx * CORES + cc) * cap, cap)],
                 recv_t.at[zs, pl.ds(mine, cap)],
-                fwd_send.at[0, zs], fwd_recv.at[0, zs], device(y, cc, z, xx),
+                fwd_send.at[0, zs], sem, device(y, cc, z, xx),
             ).start()
 
+        send(1, fwd_own.at[zs])
         pltpu.make_async_copy(
-            sbuf_t.at[zs, pl.ds(mine, cap)], recv_t.at[zs, pl.ds(mine, cap)], fwd_recv.at[0, zs]
+            sbuf_t.at[zs, pl.ds(mine, cap)], recv_t.at[zs, pl.ds(mine, cap)], fwd_own.at[zs]
         ).start()
 
-        arrived(1, cotbuf, meta_x, xs)
+        @pl.loop(CORES, line)
+        def _(q):
+            send(q, fwd_recv.at[0, zs])
+
+    def relay_cotangents(d):
+        xs = (x + d) % SIDE
+        arrived(1, cotbuf, meta_x, xs, d)
         m = meta_x[xs]
         hit0, hit1 = cot_slots == m[0:1, :], cot_slots == m[1:2, :]
         pick = jnp.where(hit0 | hit1, 1.0, 0.0).astype(BF16)
@@ -205,10 +207,10 @@
             jnp.where(hit0, m[2:3, :], 0.0) + jnp.where(hit1, m[3:4, :], 0.0), axis=1, keepdims=True
         )
 
-        @pl.loop(0, SIDE)
-        def _(n):
-            cols = pl.ds(pl.multiple_of(n * tile, tile), tile)
+        def body(cols):
             sbuf_c[xs, :, cols] = (dot(pick, cotbuf[xs, :, cols], NN) * scale).astype(BF16)
+
+        tiles(body)
 
         @pl.loop(1, line)
         def _(q):
@@ -225,23 +227,28 @@
             fwd_recv.at[1, xs],
         ).start()
 
-    wup_in.wait()
-    wdn_in.wait()
-
-    @pl.loop(0, SIDE)
-    def _(j):
-        zs = (z + step_of(j)) % SIDE
-        await_bytes(recv_t.at[zs], fwd_recv.at[0, zs])
+    def column(xs):
+        return pl.ds(pl.multiple_of(xs * pair, pair), pair)
+
+    def activate_column():
+        for d in range(SIDE):
+            zs = (z + d) % SIDE
+            await_bytes(recv_t.at[zs, column(x)], fwd_own.at[zs])
+        v = dot(recv_t[:, column(x), :].reshape(SIDE * pair, width), wu[...], NN)
+        pre[:, column(x), :] = v.reshape(SIDE, pair, hidden)
+
+    def forward(d):
+        zs = (z + d) % SIDE
+        await_bytes(recv_t.at[zs, 0 : rows - pair], fwd_recv.at[0, zs])
         v = dot(recv_t[zs], wu[...], NN)
         pre[zs] = v
-        a = (v * sigmoid(v)).astype(BF16)
-        act[zs] = a
+        act[zs] = (v * sigmoid(v)).astype(BF16)
         await_bytes(sbuf_t.at[zs, pl.ds(0, rows - cap)], fwd_send.at[0, zs])
 
-        @pl.loop(0, SIDE)
-        def _(n):
-            cols = pl.ds(pl.multiple_of(n * tile, tile), tile)
+        def body(cols):
             sbuf_t[zs, :, cols] = dot(act[zs], wd[:, cols], NN).astype(BF16)
+
+        tiles(body)
 
         @pl.loop(1, line)
         def _(q):
@@ -256,11 +263,13 @@
             sbuf_t.at[zs, pl.ds(mine, cap)], ret_o.at[zs, pl.ds(mine, cap)], bwd_recv.at[0, zs]
         ).start()
 
-    @pl.loop(0, SIDE)
-    def _(j):
-        xs = (x + step_of(j)) % SIDE
-        part = pl.ds(pl.multiple_of(xs * pair, pair), pair)
-        await_bytes(recv_c.at[:, part], fwd_recv.at[1, xs])
+    def cotangents_in(d):
+        xs = (x + d) % SIDE
+        await_bytes(recv_c.at[:, column(xs)], fwd_recv.at[1, xs])
+
+    def backward(d):
+        xs = (x + d) % SIDE
+        part = column(xs)
         da = dot(recv_c[:, part, :].reshape(rows, width), wd[...], NT)
         v = pre[:, part, :].reshape(rows, hidden)
         s = sigmoid(v)
@@ -268,11 +277,11 @@
         dpre[:, part, :] = dp_rows.reshape(SIDE, pair, hidden)
         await_bytes(sbuf_c.at[xs, pl.ds(0, rows - cap)], fwd_send.at[1, xs])
 
-        @pl.loop(0, SIDE)
-        def _(n):
-            cols = pl.ds(pl.multiple_of(n * tile, tile), tile)
+        def body(cols):
             left = dpre[:, part, :].reshape(rows, hidden)
             sbuf_c[xs, :, cols] = dot(left, wu[cols, :], NT).astype(BF16)
+
+        tiles(body)
 
         @pl.loop(1, line)
         def _(q):
@@ -287,24 +296,24 @@
             sbuf_c.at[xs, pl.ds(mine_z, cap)], ret_d.at[xs, pl.ds(mine_z, cap)], bwd_recv.at[1, xs]
         ).start()
 
-    @pl.loop(1, SIDE)
-    def _(d):
-        for k, own, metas in ((0, z, meta_z), (1, x, meta_x)):
-            await_bytes(metas.at[own], meta_send.at[k, d])
-
-    for k, buf, own in axes:
-        for side, back in ((0, SIDE - 1), (1, 1)):
-            for h in range(2):
-                await_bytes(buf.at[own, halves[h]], ag_send.at[k, side, h])
-            await_bytes(buf.at[(own + back) % SIDE, halves[side]], hand_send.at[k, side])
+    def drain():
+        @pl.loop(1, SIDE)
+        def _(d):
+            for k, own, metas in ((0, z, meta_z), (1, x, meta_x)):
+                await_bytes(metas.at[own], meta_send.at[k, d])
+
+        for k, buf, own in axes:
+            for side, back in ((0, SIDE - 1), (1, 1)):
+                for h in range(2):
+                    await_bytes(buf.at[own, halves[h]], ag_send.at[k, side, h])
+                await_bytes(buf.at[(own + back) % SIDE, halves[side]], hand_send.at[k, side])
 
     thirds = hidden // rows
-    for g, left, right, gbuf in ((0, act, recv_c, cotbuf), (1, dpre, recv_t, tokbuf)):
-
-        @pl.loop(0, SIDE)
-        def _(n, g=g, left=left, right=right, gbuf=gbuf):
-            yy = (y + step_of(SIDE - 1 - n)) % SIDE
-            cols = pl.ds(pl.multiple_of(yy * tile, tile), tile)
+
+    def weight_grad(g):
+        left, right, gbuf = ((act, recv_c, cotbuf), (dpre, recv_t, tokbuf))[g]
+
+        def body(cols):
             r = dot(
                 left[...].reshape(SIDE * rows, hidden),
                 right[:, :, cols].reshape(SIDE * rows, tile),
@@ -312,9 +321,11 @@
             )
             gbuf[0:thirds, :, cols] = r.astype(BF16).reshape(thirds, rows, tile)
 
+        tiles(body)
+
         @pl.loop(1, line)
-        def _(q, g=g, gbuf=gbuf):
-            yy, cc = y_line(line - q)
+        def _(q):
+            yy, cc = y_line(q)
             cols = pl.ds(pl.multiple_of((yy * CORES + cc) * shard, shard), shard)
             remote(
                 gbuf.at[0:thirds, :, cols], rs.at[g, c, y], rs_send.at[g], rs_recv.at[g],
@@ -323,6 +334,24 @@
 
         cols = pl.ds(pl.multiple_of((y * CORES + c) * shard, shard), shard)
         pltpu.make_async_copy(gbuf.at[0:thirds, :, cols], rs.at[g, c, y], rs_recv.at[g]).start()
+
+    def gradients_out(g):
+        await_bytes(rs.at[g], rs_recv.at[g])
+
+        @pl.loop(0, CORES)
+        def _(e):
+            total = rs[g, e, 0].astype(F32)
+            for yy in range(1, SIDE):
+                total = total + rs[g, e, yy].astype(F32)
+            if g == 0:
+                gst[e] = total.reshape(hidden, shard)
+            else:
+                pre[e] = total.reshape(hidden, shard).T
+
+        if g == 0:
+            pltpu.make_async_copy(gst, dng_hbm, out_sem.at[2]).start()
+        else:
+            pltpu.make_async_copy(pre.at[0:CORES], upg_hbm, out_sem.at[3]).start()
 
     def share(k, own, slots, metas, ret, weighted):
         def of(src, h, cols):
@@ -338,33 +367,20 @@
             return dot(high, v, TN) + dot(low, v, TN)
         return of
 
-    def tiles(body):
-        @pl.loop(0, SIDE)
-        def _(n):
-            body(pl.ds(pl.multiple_of(n * tile, tile), tile))
-
     def pass_on(k, send, got, src, h, slot, where_d):
         part = send.at[src, halves[h]]
         remote(part, got.at[slot, halves[h]], part_send.at[k, slot, h], part_recv.at[k, slot, h], near(k, where_d)).start()
 
-    def shares(k, own, slots, metas, ret, send, got, out_hbm, weighted):
+    def share_with(d, k, own, slots, metas, ret, send, got, out_hbm, weighted):
         of = share(k, own, slots, metas, ret, weighted)
-        ahead, behind, far = (own + 1) % SIDE, (own + SIDE - 1) % SIDE, (own + 2) % SIDE
-        for src, h, slot, d in ((ahead, 1, 1, 1), (behind, 0, 0, SIDE - 1)):
-            await_bytes(ret.at[src], bwd_recv.at[k, src])
-
-            def body(cols, src=src, h=h):
+        src = (own + d) % SIDE
+        await_bytes(ret.at[src], bwd_recv.at[k, src])
+        for h, slot, to in {1: ((1, 1, 1),), 3: ((0, 0, 3),), 2: ((0, 2, 1), (1, 2, 3))}[d]:
+            def body(cols, h=h):
                 send[src, halves[h], cols] = of(src, h, cols).astype(BF16)
 
             tiles(body)
-            pass_on(k, send, got, src, h, slot, d)
-        await_bytes(ret.at[far], bwd_recv.at[k, far])
-        for h, d in ((0, 1), (1, SIDE - 1)):
-            def body(cols, h=h):
-                send[far, halves[h], cols] = of(far, h, cols).astype(BF16)
-
-            tiles(body)
-            pass_on(k, send, got, far, h, 2, d)
+            pass_on(k, send, got, src, h, slot, to)
 
     def hand_on(k, own, slots, metas, ret, send, got, out_hbm, weighted):
         of = share(k, own, slots, metas, ret, weighted)
@@ -395,33 +411,40 @@
 
     fwd = (0, z, tok_slots, meta_z, ret_o, recv_t, pmr, mixed_hbm, True)
     bwd = (1, x, cot_slots, meta_x, ret_d, recv_c, pdr, igrad_hbm, False)
-    shares(*fwd)
-    shares(*bwd)
+    relay_tokens(0)
+    relay_cotangents(0)
+    hand_over()
+    for d in (1, 3, 2):
+        relay_tokens(d)
+        relay_cotangents(d)
+    wup_in.wait()
+    wdn_in.wait()
+    activate_column()
+    cotangents_in(0)
+    backward(0)
+    for d in (0, 1, 3, 2):
+        forward(d)
+    cotangents_in(2)
+    backward(2)
+    for d in (1, 3):
+        cotangents_in(d)
+    drain()
+    weight_grad(0)
+    backward(1)
+    backward(3)
+    weight_grad(1)
+    share_with(2, *bwd)
+    share_with(1, *fwd)
+    share_with(3, *fwd)
+    share_with(1, *bwd)
+    share_with(3, *bwd)
+    share_with(2, *fwd)
+    hand_on(*bwd)
+    gradients_out(0)
     hand_on(*fwd)
-    hand_on(*bwd)
+    finish(*bwd)
+    gradients_out(1)
     finish(*fwd)
-
-    await_bytes(rs.at[0], rs_recv.at[0])
-
-    @pl.loop(0, CORES)
-    def _(e):
-        total = rs[0, e, 0].astype(F32)
-        for yy in range(1, SIDE):
-            total = total + rs[0, e, yy].astype(F32)
-        gst[e] = total.reshape(hidden, shard)
-
-    pltpu.make_async_copy(gst, dng_hbm, out_sem.at[2]).start()
-    await_bytes(rs.at[1], rs_recv.at[1])
-
-    @pl.loop(0, CORES)
-    def _(e):
-        total = rs[1, e, 0].astype(F32)
-        for yy in range(1, SIDE):
-            total = total + rs[1, e, yy].astype(F32)
-        pre[e] = total.reshape(hidden, shard).T
-
-    pltpu.make_async_copy(pre.at[0:CORES], upg_hbm, out_sem.at[3]).start()
-    finish(*bwd)
 
     @pl.loop(0, SIDE)
     def _(j):
@@ -488,7 +511,7 @@
             three, three,
             pltpu.VMEM((CORES, hidden, shard), F32),
             dma((4,)), dma((2, 2, 2)), dma((2, SIDE, 2)), dma((2, 2)),
-            dma((2, SIDE)), dma((2, SIDE)),
+            dma((2, SIDE)), dma((2, SIDE)), dma((SIDE,)),
             dma((2, SIDE)), dma((2, SIDE)), dma((2, SIDE)), dma((2, SIDE)),
             dma((2,)), dma((2,)), dma((2, SIDE - 1, 2)), dma((2, SIDE - 1, 2)), dma((4,)),
         ],

time: 192 us -> 182 us (0.948)
  Pallas kernels: 192 us -> 181 us
    pallas_call x1, Pallas kernels: 187 us -> 176 us  [on_device(): pl.pallas_call(layer_kernel, out_shape=(jax.ShapeDtypeStruct((rows, width...]
where the time goes in v2:
time: 182 us; the launch traced here: 181 us
  Pallas kernels  181 us (99%)
    pallas_call x1, Pallas kernels, on_device(): pl.pallas_call(layer_kernel, out_shape=(jax.ShapeDtypeStruct((rows, width...  176 us
    pallas_call x1, Pallas kernels, on_device(): pl.pallas_call(copy_kernel, out_shape=tuple((jax.ShapeDtypeStruct(r.shape...  4.78 us

profile of v2, /device:TPU:1, one launch (start us, length us, event | category | flops | bytes accessed | tf_op | source)
XLA Modules:
  0.0 181.4 jit_solution(6893880551597492245)
XLA Ops:
  0.6 175.8 %shard_map.93 = (bf16[256,2048]{1,0:T(8,128)(2,1)}, bf16[256,2048]{1,0:T(8,128)(2,1)}, f32[2,256,768]{2,1,0:T(8,128)}, f32[2,768,256]{2,1,0:T(8,128)}) custom-call(bf16[256,2048]{1,0:T(8,128)(2,1)} %tok_hbm.1, bf16[256,2048]{1,0:T(8,128)(2,1)} %cot_hbm.1, s32[2,256]{1,0:T(2,128)} %bitcast.2, f32[2,256]{1,0:T(2,128)} %bitcast.3, ...), custom_call_target="tpu_custom_call" | custom-call | tf_op jit(solution)/shard_map/pallas_call | solution.py:492
  176.5 4.8 %shard_map.94 = (bf16[256,2048]{1,0:T(8,128)(2,1)}, bf16[256,2048]{1,0:T(8,128)(2,1)}, f32[2,256,768]{2,1,0:T(8,128)}, f32[2,768,256]{2,1,0:T(8,128)}) custom-call(bf16[256,2048]{1,0:T(8,128)(2,1)} %get-tuple-element.8.refs_0_, bf16[256,2048]{1,0:T(8,128)(2,1)} %get-tuple-element.9.refs_1_, f32[2,256,768]{2,1,0:T(8,128)} %get-tuple-element.10.refs_2_, ...), custom_call_target="tpu_custom_call" | custom-call | tf_op jit(solution)/shard_map/pallas_call | solution.py:522

commit v3 on v2

--- a/solution.py
+++ b/solution.py
@@ -25,17 +25,21 @@
     return 1.0 / (1.0 + jnp.exp(-v))
 
 
+def silu_slope(v, s):
+    return (s * (1.0 + v * (1.0 - s))).astype(BF16)
+
+
 def step_of(j):
     return j ^ (j // 2)
 
 
 def layer_kernel(
     tok_hbm, cot_hbm, routes, gates, wup_hbm, wdn_hbm,
-    mixed_hbm, igrad_hbm, upg_hbm, dng_hbm,
+    mixed, igrad, upg, dng,
     tokbuf, cotbuf, meta_z, meta_x, sbuf_t, sbuf_c, recv_t, recv_c, wu, wd,
-    pre, act, dpre, ret_o, ret_d, rs, pmr, pdr, gst,
+    act, dpre, ret_o, ret_d, rs, rs_far, pmr, pdr,
     load_sem, ag_send, ag_recv, hand_send, meta_send, meta_recv, fwd_own,
-    fwd_send, fwd_recv, bwd_send, bwd_recv, rs_send, rs_recv, part_send, part_recv, out_sem,
+    fwd_send, fwd_recv, bwd_send, bwd_recv, rs_send, rs_recv, rs_hand, part_send, part_recv,
 ):
     dp, ex = lax.axis_index("dp"), lax.axis_index("expert")
     y, c = dp // CORES, dp % CORES
@@ -59,9 +63,6 @@
     def z_line(q):
         return (z + q // CORES) % SIDE, (c + q % CORES) % CORES
 
-    def y_line(q):
-        return (y + q // CORES) % SIDE, (c + q % CORES) % CORES
-
     def remote(src, dst, ssem, rsem, where):
         return pltpu.make_async_remote_copy(
             src_ref=src, dst_ref=dst, send_sem=ssem, recv_sem=rsem,
@@ -100,8 +101,10 @@
     def _(q):
         zz, cc = z_line(q)
         greet(device(y, cc, zz, x))
-        yy, cc = y_line(q)
-        greet(device(yy, cc, z, x))
+
+    for d in (1, SIDE - 1):
+        for core in range(CORES):
+            greet(device((y + d) % SIDE, core, z, x))
 
     r0, r1 = routes[0:1, :], routes[1:2, :]
     experts = line * SIDE
@@ -121,7 +124,7 @@
     meta_z[z] = meta
     meta_x[x] = meta
 
-    pl.semaphore_wait(barrier, line - 1 + 2 * (line - CORES))
+    pl.semaphore_wait(barrier, line - 1 + line - CORES + 2 * CORES)
 
     @pl.loop(1, SIDE)
     def _(j):
@@ -235,14 +238,17 @@
             zs = (z + d) % SIDE
             await_bytes(recv_t.at[zs, column(x)], fwd_own.at[zs])
         v = dot(recv_t[:, column(x), :].reshape(SIDE * pair, width), wu[...], NN)
-        pre[:, column(x), :] = v.reshape(SIDE, pair, hidden)
+        dpre[:, column(x), :] = silu_slope(v, sigmoid(v)).reshape(SIDE, pair, hidden)
 
     def forward(d):
         zs = (z + d) % SIDE
         await_bytes(recv_t.at[zs, 0 : rows - pair], fwd_recv.at[0, zs])
         v = dot(recv_t[zs], wu[...], NN)
-        pre[zs] = v
-        act[zs] = (v * sigmoid(v)).astype(BF16)
+        s = sigmoid(v)
+        act[zs] = (v * s).astype(BF16)
+        done = dpre[zs, column(x), :]
+        dpre[zs] = silu_slope(v, s)
+        dpre[zs, column(x), :] = done
         await_bytes(sbuf_t.at[zs, pl.ds(0, rows - cap)], fwd_send.at[0, zs])
 
         def body(cols):
@@ -271,10 +277,8 @@
         xs = (x + d) % SIDE
         part = column(xs)
         da = dot(recv_c[:, part, :].reshape(rows, width), wd[...], NT)
-        v = pre[:, part, :].reshape(rows, hidden)
-        s = sigmoid(v)
-        dp_rows = (da * s * (1.0 + v * (1.0 - s))).astype(BF16)
-        dpre[:, part, :] = dp_rows.reshape(SIDE, pair, hidden)
+        slope = dpre[:, part, :].reshape(rows, hidden).astype(F32)
+        dpre[:, part, :] = (da * slope).astype(BF16).reshape(SIDE, pair, hidden)
         await_bytes(sbuf_c.at[xs, pl.ds(0, rows - cap)], fwd_send.at[1, xs])
 
         def body(cols):
@@ -310,10 +314,21 @@
 
     thirds = hidden // rows
 
+    def grad_cols(d, core):
+        return pl.ds(pl.multiple_of(((y + d) % SIDE * CORES + core) * shard, shard), shard)
+
+    def send_grad(g, d, core, dst, sem, where):
+        gbuf = (cotbuf, tokbuf)[g]
+        remote(gbuf.at[0:thirds, :, grad_cols(d, core)], dst, rs_send.at[g], sem, where).start()
+
     def weight_grad(g):
         left, right, gbuf = ((act, recv_c, cotbuf), (dpre, recv_t, tokbuf))[g]
-
-        def body(cols):
+        ahead, behind = (y + 1) % SIDE, (y + SIDE - 1) % SIDE
+
+        @pl.loop(0, SIDE)
+        def _(n):
+            yy = (y + 2 + n) % SIDE
+            cols = pl.ds(pl.multiple_of(yy * tile, tile), tile)
             r = dot(
                 left[...].reshape(SIDE * rows, hidden),
                 right[:, :, cols].reshape(SIDE * rows, tile),
@@ -321,19 +336,27 @@
             )
             gbuf[0:thirds, :, cols] = r.astype(BF16).reshape(thirds, rows, tile)
 
-        tiles(body)
-
-        @pl.loop(1, line)
-        def _(q):
-            yy, cc = y_line(q)
-            cols = pl.ds(pl.multiple_of((yy * CORES + cc) * shard, shard), shard)
-            remote(
-                gbuf.at[0:thirds, :, cols], rs.at[g, c, y], rs_send.at[g], rs_recv.at[g],
-                device(yy, cc, z, x),
-            ).start()
-
-        cols = pl.ds(pl.multiple_of((y * CORES + c) * shard, shard), shard)
-        pltpu.make_async_copy(gbuf.at[0:thirds, :, cols], rs.at[g, c, y], rs_recv.at[g]).start()
+            @pl.when(n == 0)
+            def _():
+                send_grad(g, 2, 0, rs_far.at[g, 0], rs_hand.at[g, 0], device(ahead, c, z, x))
+                send_grad(g, 2, 1, rs_far.at[g, 1], rs_hand.at[g, 1], device(behind, c, z, x))
+
+        send_grad(g, 1, 1, rs.at[g, c, 1], rs_recv.at[g], device(ahead, 1, z, x))
+        send_grad(g, SIDE - 1, 0, rs.at[g, c, 0], rs_recv.at[g], device(behind, 0, z, x))
+        send_grad(g, 0, 1 - c, rs.at[g, c, 2], rs_recv.at[g], device(y, 1 - c, z, x))
+        pltpu.make_async_copy(
+            gbuf.at[0:thirds, :, grad_cols(0, c)], rs.at[g, c, 2], rs_recv.at[g]
+        ).start()
+
+    def hand_on_grad(g):
+        gbuf = (cotbuf, tokbuf)[g]
+        for h, d, slot in ((0, 1, 1), (1, SIDE - 1, 0)):
+            await_bytes(rs_far.at[g, h], rs_hand.at[g, h])
+            cols = grad_cols(d, h)
+            gbuf[0:thirds, :, cols] = (
+                gbuf[0:thirds, :, cols].astype(F32) + rs_far[g, h].astype(F32)
+            ).astype(BF16)
+            send_grad(g, d, h, rs.at[g, c, slot], rs_recv.at[g], device((y + d) % SIDE, h, z, x))
 
     def gradients_out(g):
         await_bytes(rs.at[g], rs_recv.at[g])
@@ -341,17 +364,12 @@
         @pl.loop(0, CORES)
         def _(e):
             total = rs[g, e, 0].astype(F32)
-            for yy in range(1, SIDE):
-                total = total + rs[g, e, yy].astype(F32)
+            for part in range(1, SIDE - 1):
+                total = total + rs[g, e, part].astype(F32)
             if g == 0:
-                gst[e] = total.reshape(hidden, shard)
+                dng[e] = total.reshape(hidden, shard)
             else:
-                pre[e] = total.reshape(hidden, shard).T
-
-        if g == 0:
-            pltpu.make_async_copy(gst, dng_hbm, out_sem.at[2]).start()
-        else:
-            pltpu.make_async_copy(pre.at[0:CORES], upg_hbm, out_sem.at[3]).start()
+                upg[e] = total.reshape(hidden, shard).T
 
     def share(k, own, slots, metas, ret, weighted):
         def of(src, h, cols):
@@ -371,7 +389,7 @@
         part = send.at[src, halves[h]]
         remote(part, got.at[slot, halves[h]], part_send.at[k, slot, h], part_recv.at[k, slot, h], near(k, where_d)).start()
 
-    def share_with(d, k, own, slots, metas, ret, send, got, out_hbm, weighted):
+    def share_with(d, k, own, slots, metas, ret, send, got, out, weighted):
         of = share(k, own, slots, metas, ret, weighted)
         src = (own + d) % SIDE
         await_bytes(ret.at[src], bwd_recv.at[k, src])
@@ -382,7 +400,7 @@
             tiles(body)
             pass_on(k, send, got, src, h, slot, to)
 
-    def hand_on(k, own, slots, metas, ret, send, got, out_hbm, weighted):
+    def hand_on(k, own, slots, metas, ret, send, got, out, weighted):
         of = share(k, own, slots, metas, ret, weighted)
         ahead, behind = (own + 1) % SIDE, (own + SIDE - 1) % SIDE
         for src, h, slot, d in ((ahead, 0, 1, 1), (behind, 1, 0, SIDE - 1)):
@@ -395,25 +413,32 @@
             tiles(body)
             pass_on(k, send, got, src, h, slot, d)
 
-    def finish(k, own, slots, metas, ret, send, got, out_hbm, weighted):
+    def own_share(k, own, slots, metas, ret, send, got, out, weighted):
         of = share(k, own, slots, metas, ret, weighted)
         await_bytes(ret.at[own], bwd_recv.at[k, own])
-        for slot in range(2):
+
+        def body(cols):
             for h in range(2):
+                send[own, halves[h], cols] = of(own, h, cols).astype(BF16)
+
+        tiles(body)
+
+    def finish(k, own, slots, metas, ret, send, got, out, weighted):
+        for h in ((0, 1), (1, 0))[k]:
+            for slot in range(2):
                 await_bytes(got.at[slot, halves[h]], part_recv.at[k, slot, h])
-        for h in range(2):
-            def body(cols, h=h):
-                total = of(own, h, cols) + got[0, halves[h], cols].astype(F32)
-                send[own, halves[h], cols] = (total + got[1, halves[h], cols].astype(F32)).astype(BF16)
-
-            tiles(body)
-        pltpu.make_async_copy(send.at[own], out_hbm, out_sem.at[k]).start()
-
-    fwd = (0, z, tok_slots, meta_z, ret_o, recv_t, pmr, mixed_hbm, True)
-    bwd = (1, x, cot_slots, meta_x, ret_d, recv_c, pdr, igrad_hbm, False)
+
+        @pl.loop(0, rows // 32)
+        def _(n):
+            part = pl.ds(pl.multiple_of(n * 32, 32), 32)
+            total = send[own, part, :].astype(F32) + got[0, part, :].astype(F32)
+            out[part, :] = (total + got[1, part, :].astype(F32)).astype(BF16)
+
+    fwd = (0, z, tok_slots, meta_z, ret_o, recv_t, pmr, mixed, True)
+    bwd = (1, x, cot_slots, meta_x, ret_d, recv_c, pdr, igrad, False)
+    hand_over()
     relay_tokens(0)
     relay_cotangents(0)
-    hand_over()
     for d in (1, 3, 2):
         relay_tokens(d)
         relay_cotangents(d)
@@ -434,14 +459,18 @@
     backward(3)
     weight_grad(1)
     share_with(2, *bwd)
+    hand_on_grad(0)
     share_with(1, *fwd)
     share_with(3, *fwd)
     share_with(1, *bwd)
     share_with(3, *bwd)
+    hand_on_grad(1)
     share_with(2, *fwd)
+    own_share(*bwd)
     hand_on(*bwd)
     gradients_out(0)
     hand_on(*fwd)
+    own_share(*fwd)
     finish(*bwd)
     gradients_out(1)
     finish(*fwd)
@@ -458,26 +487,6 @@
 
     for g, gbuf in ((0, cotbuf), (1, tokbuf)):
         await_bytes(gbuf.at[0:thirds, :, 0 : width - shard], rs_send.at[g])
-
-    pltpu.make_async_copy(recv_t.at[z], mixed_hbm, out_sem.at[0]).wait()
-    pltpu.make_async_copy(recv_c.at[x], igrad_hbm, out_sem.at[1]).wait()
-    pltpu.make_async_copy(gst, dng_hbm, out_sem.at[2]).wait()
-    pltpu.make_async_copy(pre.at[0:CORES], upg_hbm, out_sem.at[3]).wait()
-
-
-def copy_kernel(*refs):
-    srcs, dsts, bufs, sem = refs[0:4], refs[4:8], refs[8:12], refs[12]
-    pieces = []
-    for i in range(4):
-        first = srcs[i].shape[0] // 2
-        pieces += [(i, h, pl.ds(h * first, first)) for h in range(2)]
-    for i, h, part in pieces:
-        pltpu.make_async_copy(srcs[i].at[part], bufs[i].at[part], sem.at[0, i, h]).start()
-    for i, h, part in pieces:
-        pltpu.make_async_copy(srcs[i].at[part], bufs[i].at[part], sem.at[0, i, h]).wait()
-        pltpu.make_async_copy(bufs[i].at[part], dsts[i].at[part], sem.at[1, i, h]).start()
-    for i, h, part in pieces:
-        pltpu.make_async_copy(bufs[i].at[part], dsts[i].at[part], sem.at[1, i, h]).wait()
 
 
 def on_device(tokens, routes, gate_weights, w_up, w_down, cotangent):
@@ -489,43 +498,36 @@
     four = pltpu.VMEM((SIDE, rows, width), BF16)
     three = pltpu.VMEM((SIDE - 1, rows, width), BF16)
     dma = pltpu.SemaphoreType.DMA
+    shapes = (
+        ((rows, width), BF16), ((rows, width), BF16),
+        ((held, shard, hidden), F32), ((held, hidden, shard), F32),
+    )
     results = pl.pallas_call(
         layer_kernel,
-        out_shape=(
-            jax.ShapeDtypeStruct((rows, width), BF16),
-            jax.ShapeDtypeStruct((rows, width), BF16),
-            jax.ShapeDtypeStruct((held, shard, hidden), F32),
-            jax.ShapeDtypeStruct((held, hidden, shard), F32),
-        ),
+        out_shape=tuple(pltpu.VMEM(*r) for r in shapes),
         in_specs=[hbm, hbm, vmem, vmem, hbm, hbm],
-        out_specs=(hbm, hbm, hbm, hbm),
+        out_specs=(vmem,) * 4,
         scratch_shapes=[
             four, four,
             pltpu.VMEM((SIDE, 8, rows), F32), pltpu.VMEM((SIDE, 8, rows), F32),
             four, four, four, four,
             pltpu.VMEM((width, hidden), BF16), pltpu.VMEM((hidden, width), BF16),
-            pltpu.VMEM((SIDE, rows, hidden), F32),
             pltpu.VMEM((SIDE, rows, hidden), BF16), pltpu.VMEM((SIDE, rows, hidden), BF16),
             four, four,
-            pltpu.VMEM((2, CORES, SIDE, hidden // rows, rows, shard), BF16),
+            pltpu.VMEM((2, CORES, SIDE - 1, hidden // rows, rows, shard), BF16),
+            pltpu.VMEM((2, CORES, hidden // rows, rows, shard), BF16),
             three, three,
-            pltpu.VMEM((CORES, hidden, shard), F32),
             dma((4,)), dma((2, 2, 2)), dma((2, SIDE, 2)), dma((2, 2)),
             dma((2, SIDE)), dma((2, SIDE)), dma((SIDE,)),
             dma((2, SIDE)), dma((2, SIDE)), dma((2, SIDE)), dma((2, SIDE)),
-            dma((2,)), dma((2,)), dma((2, SIDE - 1, 2)), dma((2, SIDE - 1, 2)), dma((4,)),
+            dma((2,)), dma((2,)), dma((2, CORES)),
+            dma((2, SIDE - 1, 2)), dma((2, SIDE - 1, 2)),
         ],
         compiler_params=pltpu.CompilerParams(
-            collective_id=0, has_side_effects=True, vmem_limit_bytes=63 << 20
+            collective_id=0, has_side_effects=True, vmem_limit_bytes=58 << 20
         ),
     )(tokens, cotangent, routes.T, gate_weights.T, w_up, w_down)
-    return pl.pallas_call(
-        copy_kernel,
-        out_shape=tuple(jax.ShapeDtypeStruct(r.shape, r.dtype) for r in results),
-        in_specs=[hbm] * 4,
-        out_specs=(hbm,) * 4,
-        scratch_shapes=[pltpu.VMEM(r.shape, r.dtype) for r in results] + [dma((2, 4, 2))],
-    )(*results)
+    return results
 
 
 def solution(mesh):

time: 182 us -> 176 us (0.967)
  Pallas kernels: 181 us -> 171 us
  local copies, waits for them, and re-layouts: 0 us -> 4.23 us
    pallas_call x2 -> x1, Pallas kernels: 181 us -> 171 us  [on_device(): pl.pallas_call(layer_kernel, out_shape=tuple((pltpu.VMEM(*r) for r in sha...]
    unnamed x0 -> x4, local copies, waits for them, and re-layouts: none -> 4.23 us
where the time goes in v3:
time: 176 us
  Pallas kernels  171 us (97%)
  local copies, waits for them, and re-layouts  4.23 us (2%)
    pallas_call x1, Pallas kernels, on_device(): pl.pallas_call(layer_kernel, out_shape=tuple((pltpu.VMEM(*r) for r in sha...  171 us
    unnamed x4, local copies, waits for them, and re-layouts  4.23 us

profile of v3, /device:TPU:1, one launch (start us, length us, event | category | flops | bytes accessed | tf_op | source)
XLA Modules:
  0.0 176.0 jit_solution(14080691960737720500)
XLA Ops:
  0.6 171.1 %shard_map.93 = (bf16[256,2048]{1,0:T(8,128)(2,1)S(1)}, bf16[256,2048]{1,0:T(8,128)(2,1)S(1)}, f32[2,256,768]{2,1,0:T(8,128)S(1)}, f32[2,768,256]{2,1,0:T(8,128)S(1)}) custom-call(bf16[256,2048]{1,0:T(8,128)(2,1)} %tok_hbm.1, bf16[256,2048]{1,0:T(8,128)(2,1)} %cot_hbm.1, s32[2,256]{1,0:T(2,128)} %bitcast.2, f32[2,256]{1,0:T(2,128)} %bitcast.3, ...), custom_call_target="tpu_custom_call" | custom-call | tf_op jit(solution)/shard_map/pallas_call | solution.py:505
  171.7 1.0 copy.14
  172.7 1.0 copy.15
  173.7 1.1 copy.16
  174.8 1.1 copy.17

commit v4 on v3

--- a/solution.py
+++ b/solution.py
@@ -126,13 +126,6 @@
 
     pl.semaphore_wait(barrier, line - 1 + line - CORES + 2 * CORES)
 
-    @pl.loop(1, SIDE)
-    def _(j):
-        d = step_of(j)
-        to_z, to_x = device(y, c, (z + d) % SIDE, x), device(y, c, z, (x + d) % SIDE)
-        remote(meta_z.at[z], meta_z.at[z], meta_send.at[0, d], meta_recv.at[0, z], to_z).start()
-        remote(meta_x.at[x], meta_x.at[x], meta_send.at[1, d], meta_recv.at[1, x], to_x).start()
-
     tok_in.wait()
     cot_in.wait()
 
@@ -143,6 +136,13 @@
                 h = side if first else 1 - side
                 part = buf.at[own, halves[h]]
                 remote(part, part, ag_send.at[k, side, h], ag_recv.at[k, own, h], near(k, d)).start()
+
+    @pl.loop(1, SIDE)
+    def _(j):
+        d = step_of(j)
+        to_z, to_x = device(y, c, (z + d) % SIDE, x), device(y, c, z, (x + d) % SIDE)
+        remote(meta_z.at[z], meta_z.at[z], meta_send.at[0, d], meta_recv.at[0, z], to_z).start()
+        remote(meta_x.at[x], meta_x.at[x], meta_send.at[1, d], meta_recv.at[1, x], to_x).start()
 
     wup_in.start()
     wdn_in.start()
@@ -489,6 +489,20 @@
         await_bytes(gbuf.at[0:thirds, :, 0 : width - shard], rs_send.at[g])
 
 
+def copy_kernel(*refs):
+    srcs, dsts, sem = refs[0:4], refs[4:8], refs[8]
+    copies = []
+    for i in range(4):
+        first = srcs[i].shape[0] // 2
+        for h in range(2):
+            part = pl.ds(h * first, first)
+            copies.append(pltpu.make_async_copy(srcs[i].at[part], dsts[i].at[part], sem.at[i, h]))
+    for copy in copies:
+        copy.start()
+    for copy in copies:
+        copy.wait()
+
+
 def on_device(tokens, routes, gate_weights, w_up, w_down, cotangent):
     rows, width = tokens.shape
     held, _, hidden = w_up.shape
@@ -527,7 +541,14 @@
             collective_id=0, has_side_effects=True, vmem_limit_bytes=58 << 20
         ),
     )(tokens, cotangent, routes.T, gate_weights.T, w_up, w_down)
-    return results
+    return pl.pallas_call(
+        copy_kernel,
+        out_shape=tuple(jax.ShapeDtypeStruct(*r) for r in shapes),
+        in_specs=[vmem] * 4,
+        out_specs=(hbm,) * 4,
+        scratch_shapes=[dma((4, 2))],
+        compiler_params=pltpu.CompilerParams(vmem_limit_bytes=8 << 20),
+    )(*(pltpu.with_memory_space_constraint(r, pltpu.VMEM) for r in results))
 
 
 def solution(mesh):

time: 176 us -> 174 us (0.989)
  local copies, waits for them, and re-layouts: 4.23 us -> 0 us
  Pallas kernels: 171 us -> 174 us
    unnamed x4 -> x0, local copies, waits for them, and re-layouts: 4.23 us -> none
    pallas_call x0 -> x1, Pallas kernels: none -> 2.42 us  [on_device(): pl.pallas_call(copy_kernel, out_shape=tuple((jax.ShapeDtypeStruct(*r) for...]
where the time goes in v4:
time: 174 us
  Pallas kernels  174 us (100%)
    pallas_call x1, Pallas kernels, on_device(): pl.pallas_call(layer_kernel, out_shape=tuple((pltpu.VMEM(*r) for r in sha...  171 us

profile of v4, /device:TPU:1, one launch (start us, length us, event | category | flops | bytes accessed | tf_op | source)
XLA Modules:
  0.0 174.3 jit_solution(8912139090179048419)
XLA Ops:
  0.6 171.1 %shard_map.93 = (bf16[256,2048]{1,0:T(8,128)(2,1)S(1)}, bf16[256,2048]{1,0:T(8,128)(2,1)S(1)}, f32[2,256,768]{2,1,0:T(8,128)S(1)}, f32[2,768,256]{2,1,0:T(8,128)S(1)}) custom-call(bf16[256,2048]{1,0:T(8,128)(2,1)} %tok_hbm.1, bf16[256,2048]{1,0:T(8,128)(2,1)} %cot_hbm.1, s32[2,256]{1,0:T(2,128)} %bitcast.2, f32[2,256]{1,0:T(2,128)} %bitcast.3, ...), custom_call_target="tpu_custom_call" | custom-call | tf_op jit(solution)/shard_map/pallas_call | solution.py:519
  171.7 2.4 %shard_map.94 = (bf16[256,2048]{1,0:T(8,128)(2,1)}, bf16[256,2048]{1,0:T(8,128)(2,1)}, f32[2,256,768]{2,1,0:T(8,128)}, f32[2,768,256]{2,1,0:T(8,128)}) custom-call(bf16[256,2048]{1,0:T(8,128)(2,1)S(1)} %get-tuple-element.8.refs_0_, bf16[256,2048]{1,0:T(8,128)(2,1)S(1)} %get-tuple-element.9.refs_1_, f32[2,256,768]{2,1,0:T(8,128)S(1)} %get-tuple-element.10.refs_2_, ...), custom_call_target="tpu_custom_call" | custom-call | tf_op jit(solution)/shard_map/pallas_call | solution.py:544
